TPU v7x, 32 devices: a whole 2x2x4 slice. The times are simulated.
32 devices in a mesh: row: 4 (over x, core), col: 8 (over z, y).
Axes of the slice: x: 2, y: 2, z: 4, core: 2. Of those that a mesh axis runs over, the one named last changes fastest.
Arguments:
- weight: bfloat16 [16384, 16384], P('row', 'col'), may hold values from -0.046875 to 0.046875
- momentum: float32 [16384, 16384], P('row', 'col'), may hold values from -36 to 36
- right_factor: float32 [16384, 512], P(('col', 'row')), may hold values from -0.046875 to 0.046875
- output_grads: bfloat16 [1024, 16384], P('col', 'row'), may hold values from -0.1875 to 0.1875
- activations: bfloat16 [1024, 16384], P('row', 'col'), may hold values from -6 to 6
Outputs:
- new_weight: bfloat16 [16384, 16384], P('row', 'col')
- new_momentum: float32 [16384, 16384], P('row', 'col')
- new_factor: float32 [16384, 512], P(('col', 'row'))
All inputs are finite; a program needn't handle non-finite values.
Results may differ from a plain program's by a relative error of at most 0.0004.
Values may be sent and summed in bfloat16 or wider, within the bound.
No kernel may reach another device: no remote copies, remote signals or barrier semaphores. Data moves between devices by JAX's collectives and lax.ppermute only.
A program may use at most 192 MiB of HBM per device.

v0:
```python
import math
import jax
import jax.numpy as jnp
from jax import lax
from jax.sharding import PartitionSpec as P

D_OUT = 16384
D_IN = 16384
FULL_PRECISION = lax.Precision.HIGHEST
MOMENTUM_DECAY = 0.95
LEARN_RATE = 0.002
NORM_EPS = 1e-06


def contract_rows(first, second):
    return lax.dot_general(
        first,
        second,
        (((0,), (0,)), ((), ())),
        precision=FULL_PRECISION,
        preferred_element_type=jnp.float32,
    )


def outer_rows(first, second):
    return lax.dot_general(
        first,
        second,
        (((1,), (1,)), ((), ())),
        precision=FULL_PRECISION,
        preferred_element_type=jnp.float32,
    )


def orthogonalize(left_factor, gram_matrix):
    lower_factor = jnp.linalg.cholesky(gram_matrix)
    identity = jnp.eye(gram_matrix.shape[0], dtype=gram_matrix.dtype)
    inverse = jax.scipy.linalg.solve_triangular(lower_factor, identity, lower=True)
    return outer_rows(left_factor, inverse)


def body(weight, momentum, right_factor, output_grads, activations):
    grads_whole = lax.all_gather(output_grads, "col", axis=0, tiled=True)
    grad_tile = lax.dot_general(
        grads_whole,
        lax.all_gather(activations, "row", axis=0, tiled=True),
        (((0,), (0,)), ((), ())),
        preferred_element_type=jnp.float32,
    )
    buffer = momentum + grad_tile
    factor_block = lax.all_gather(right_factor, "row", axis=0, tiled=True)
    left_partial = jnp.dot(
        buffer, factor_block, precision=FULL_PRECISION, preferred_element_type=jnp.float32
    )
    left_factor = lax.psum(left_partial, "col")
    gram_matrix = lax.psum(contract_rows(left_factor, left_factor), "row")
    ortho_left = orthogonalize(left_factor, gram_matrix)
    right_piece = lax.psum_scatter(
        contract_rows(buffer, ortho_left), "row", scatter_dimension=0, tiled=True
    )
    column_squares = lax.psum(jnp.sum(right_piece * right_piece, axis=0), ("row", "col"))
    column_norm = jnp.sqrt(column_squares + NORM_EPS)
    new_factor = right_piece / column_norm
    projected = lax.all_gather(right_piece, "row", axis=0, tiled=True)
    new_momentum = buffer - (1.0 - MOMENTUM_DECAY) * outer_rows(ortho_left, projected)
    factor_cols = projected / column_norm
    step_scale = LEARN_RATE * math.sqrt(max(D_OUT, D_IN))
    new_weight = (
        weight.astype(jnp.float32) - step_scale * outer_rows(ortho_left, factor_cols)
    ).astype(jnp.bfloat16)
    return (new_weight, new_momentum, new_factor)


def solution(mesh):
    in_specs = (
        P("row", "col"),
        P("row", "col"),
        P(("col", "row"), None),
        P("col", "row"),
        P("row", "col"),
    )
    out_specs = (P("row", "col"), P("row", "col"), P(("col", "row"), None))
    return jax.shard_map(body, mesh=mesh, in_specs=in_specs, out_specs=out_specs, check_vma=False)
```

profile of v0, /device:TPU:0, one launch (start us, length us, event | category | flops | bytes accessed | tf_op | source)
XLA Modules:
  0.0 1043.1 jit_solution(17681060143477142184)
XLA Ops:
  9.4 37.3 %all-gather.7.cloned.1.call-done = bf16[1024,2048]{1,0:T(8,128)(2,1)} async-done(((bf16[256,2048]{1,0:T(8,128)(2,1)}), bf16[1024,2048]{1,0:T(8,128)(2,1)}) %all-gather.7.cloned.1.call-update) | async-done | bytes 4194320 | tf_op jit(solution)/shard_map/all_gather | solution.py:46
  46.7 126.6 %all-gather.5.cloned.1.call-done = bf16[1024,4096]{1,0:T(8,128)(2,1)} async-done(((bf16[128,4096]{1,0:T(8,128)(2,1)}), bf16[1024,4096]{1,0:T(8,128)(2,1)}) %all-gather.5.cloned.1.call-update) | async-done | bytes 8388624 | tf_op jit(solution)/shard_map/all_gather | solution.py:43
  173.4 36.2 %convolution_add_fusion = f32[4096,2048]{1,0:T(8,128)} fusion(f32[4096,2048]{1,0:T(8,128)} %param.6, bf16[1024,4096]{1,0:T(8,128)(2,1)} %all-gather.5.cloned.1.call-done, bf16[1024,2048]{1,0:T(8,128)(2,1)} %all-gather.7.cloned.1.call-done), kind=kOutput, calls=%fused_computation.4 | convolution fusion | flops 17188257792 | bytes 79691776 | tf_op jit(solution)/shard_map/dot_general | solution.py:44
  209.6 65.1 %fusion.43 = f32[4096,512]{1,0:T(8,128)} fusion(f32[4096,2048]{1,0:T(8,128)} %convolution_add_fusion, f32[2048,512]{1,0:T(8,128)} %all-gather.9.cloned.1.call-done), kind=kOutput, calls=%fused_computation.85 | convolution fusion | flops 51539607552 | bytes 46137344 | tf_op jit(solution)/shard_map/dot_general | solution.py:52
  275.0 267.8 %all-reduce.4.cloned.1.call-done = f32[4096,512]{1,0:T(8,128)} async-done(((f32[4096,512]{1,0:T(8,128)}), f32[4096,512]{1,0:T(8,128)}) %all-reduce.4.cloned.1.call-update) | async-done | bytes 8388624 | tf_op jit(solution)/shard_map/psum | solution.py:55
  542.8 18.5 %fusion.44 = f32[512,512]{0,1:T(8,128)} fusion(f32[4096,512]{1,0:T(8,128)} %all-reduce.4.cloned.1.call-done), kind=kOutput, calls=%fused_computation.86 | convolution fusion | flops 12884901888 | bytes 9437184 | tf_op jit(solution)/shard_map/dot_general | solution.py:16
  562.3 34.6 %all-reduce.6.cloned.1.call-done = f32[512,512]{0,1:T(8,128)} async-done(((f32[512,512]{0,1:T(8,128)}), f32[512,512]{0,1:T(8,128)}) %all-reduce.6.cloned.1.call-update) | async-done | bytes 1048592 | tf_op jit(solution)/shard_map/psum | solution.py:56
  599.9 11.7 %cholesky.104 = f32[128,128]{1,0:T(8,128)S(1)} custom-call(f32[128,128]{1,0:T(8,128)S(1)} %cholesky.266), custom_call_target="Cholesky" | custom-call | tf_op jit(solution)/shard_map/jit(cholesky)/cholesky | solution.py:36
  611.7 9.8 custom-call.31
  622.3 11.7 %cholesky.217 = f32[128,128]{1,0:T(8,128)S(1)} custom-call(f32[128,128]{1,0:T(8,128)S(1)} %cholesky.270), custom_call_target="Cholesky" | custom-call | tf_op jit(solution)/shard_map/jit(cholesky)/cholesky | solution.py:36
  634.0 18.5 %custom-call.32 = f32[1,128,128]{1,2,0:T(8,128)S(1)} custom-call(f32[1,128,128]{2,1,0:T(8,128)S(1)} %get-tuple-element.27), custom_call_target="InvertDiagBlocksLowerTriangular" | custom-call | tf_op jit(solution)/shard_map/jit(cholesky)/cholesky | solution.py:36
  653.2 11.7 %cholesky.238 = f32[128,128]{1,0:T(8,128)S(1)} custom-call(f32[128,128]{1,0:T(8,128)S(1)} %cholesky.275), custom_call_target="Cholesky" | custom-call | tf_op jit(solution)/shard_map/jit(cholesky)/cholesky | solution.py:36
  665.6 9.8 custom-call.33
  676.0 11.7 %cholesky.255 = f32[128,128]{1,0:T(8,128)S(1)} custom-call(f32[128,128]{1,0:T(8,128)S(1)} %convolution_subtract_fusion.5), custom_call_target="Cholesky" | custom-call | tf_op jit(solution)/shard_map/jit(cholesky)/cholesky | solution.py:36
  692.0 10.1 while.1
  702.1 40.1 %custom-call.34 = f32[4,128,128]{1,2,0:T(8,128)S(1)} custom-call(f32[4,128,128]{2,1,0:T(8,128)} %get-tuple-element.10), custom_call_target="InvertDiagBlocksLowerTriangular" | custom-call | tf_op jit(solution)/shard_map/jit(_solve_triangular)/triangular_solve | solution.py:38
  746.0 17.1 %fusion.2 = f32[4096,512]{1,0:T(8,128)S(1)} fusion(f32[4096,512]{1,0:T(8,128)} %all-reduce.4.cloned.1.call-done, f32[128,512]{1,0:T(8,128)S(1)} %fusion.30, f32[128,512]{1,0:T(8,128)S(1)} %fusion.31, f32[128,512]{1,0:T(8,128)S(1)} %fusion.33, f32[128,512]{1,0:T(8,128)S(1)} %fusion.21), kind=kOutput, calls=%fused_computation.16 | convolution fusion | flops 12885688320 | bytes 17825792 | tf_op jit(solution)/shard_map/dot_general | solution.py:26
  763.2 3.2 copy-done
  766.4 58.7 %fusion.45 = f32[2048,512]{1,0:T(8,128)} fusion(f32[4096,2048]{1,0:T(8,128)} %convolution_add_fusion, f32[4096,512]{1,0:T(8,128)S(1)} %fusion.2), kind=kOutput, calls=%fused_computation.87 | convolution fusion | flops 51539607552 | bytes 46137344 | tf_op jit(solution)/shard_map/dot_general | solution.py:16
  825.2 45.2 %reduce-scatter.2.cloned.1.call-done = f32[512,512]{1,0:T(8,128)} async-done(((f32[2048,512]{1,0:T(8,128)}), f32[512,512]{1,0:T(8,128)}) %reduce-scatter.2.cloned.1.call-update) | async-done | bytes 1048592 | tf_op jit(solution)/shard_map/reduce_scatter | solution.py:58
  871.7 39.7 %psum.23 = f32[512]{0:T(512)S(1)} all-reduce(f32[512]{0:T(512)S(1)} %multiply_reduce_fusion), channel_id=1, replica_groups=mesh['row'=4,'col'=8] {'row','col'}, use_global_device_ids=true, to_apply=%region_12.13 | all-reduce | flops 512 | bytes 4096 | tf_op jit(solution)/shard_map/psum | solution.py:61
  911.4 2.3 broadcast_divide_fusion
  913.8 62.5 %multiply_subtract_fusion = f32[4096,2048]{1,0:T(8,128)} fusion(f32[4096,2048]{1,0:T(8,128)} %convolution_add_fusion, f32[4096,512]{1,0:T(8,128)} %copy-done, f32[2048,512]{1,0:T(8,128)} %all-gather.11.cloned.1.call-done), kind=kOutput, calls=%fused_computation.2 | convolution fusion | flops 51556384768 | bytes 79691776 | tf_op jit(solution)/shard_map/dot_general | solution.py:26
  976.3 59.6 %subtract_convert_fusion = bf16[4096,2048]{1,0:T(8,128)(2,1)} fusion(bf16[4096,2048]{1,0:T(8,128)(2,1)} %param.5, f32[4096,512]{1,0:T(8,128)} %copy-done, f32[2048,512]{1,0:T(8,128)S(1)} %copy-done.1, f32[512]{0:T(512)S(1)} %add_sqrt_fusion), kind=kOutput, calls=%fused_computation.3 | convolution fusion | flops 51574210560 | bytes 46139392 | tf_op jit(solution)/shard_map/dot_general | solution.py:26
  (65 shorter events, 26.3 us)
Async XLA Ops:
  7.2 39.6 %all-gather.7.cloned.1.call-start = ((), (), s32[]{:S(2)}) async-start(), calls=%async_computation.2 | async-start | bytes 5242880 | tf_op jit(solution)/shard_map/all_gather | solution.py:46
  7.9 165.5 %all-gather.5.cloned.1.call-start = ((), (), s32[]{:S(2)}) async-start(), calls=%async_computation.1 | async-start | bytes 9437184 | tf_op jit(solution)/shard_map/all_gather | solution.py:43
  8.6 201.0 %all-gather.9.cloned.1.call-start = ((), (), s32[]{:S(2)}) async-start(), calls=%async_computation.3 | async-start | bytes 5242880 | tf_op jit(solution)/shard_map/all_gather | solution.py:51
  9.4 533.4 %all-reduce.4.cloned.1.call-start = ((), (), s32[]{:S(2)}) async-start(), calls=%async_computation.4 | async-start | bytes 16777216 | tf_op jit(solution)/shard_map/psum | solution.py:55
  274.7 322.2 %all-reduce.6.cloned.1.call-start = ((), (), s32[]{:S(2)}) async-start(), calls=%async_computation.5 | async-start | bytes 2097152 | tf_op jit(solution)/shard_map/psum | solution.py:56
  561.3 309.0 %reduce-scatter.2.cloned.1.call-start = ((), (), s32[]{:S(2)}) async-start(), calls=%async_computation.6 | async-start | bytes 5242880 | tf_op jit(solution)/shard_map/reduce_scatter | solution.py:58
  763.2 3.2 copy-start
  825.1 88.6 %all-gather.11.cloned.1.call-start = ((), (), s32[]{:S(2)}) async-start(), calls=%async_computation.7 | async-start | bytes 5242880 | tf_op jit(solution)/shard_map/all_gather | solution.py:64
  913.8 62.5 %copy-start.1 = (f32[2048,512]{1,0:T(8,128)S(1)}, f32[2048,512]{1,0:T(8,128)}, u32[]{:S(2)}) copy-start(f32[2048,512]{1,0:T(8,128)} %all-gather.11.cloned.1.call-done) | copy-start | bytes 12582916
Sparse Core Ops, SparseCore 0:
  9.5 37.1 all-gather.6
  48.9 124.4 all-gather.4
  174.9 32.6 all-gather.8
  274.8 267.9 all-reduce.3
  561.5 35.3 all-reduce.5
  825.3 45.0 reduce-scatter.1
  871.9 34.7 all-gather.10
where the time goes:
time: 1050 us; the launch traced here: 1040 us
  waiting for transfers between devices  514 us (49%)
  matrix products  323 us (31%)
  other arithmetic  134 us (13%)
  blocking collectives  39.7 us (4%)
  between operations  17.2 us (2%)
  local copies, waits for them, and re-layouts  15 us (1%)
    psum x1, waiting for transfers between devices, body(): left_factor = lax.psum(left_partial, 'col')  268 us
    dot_general x3, matrix products, outer_rows(): lax.dot_general(first, second, (((1,), (1,)), ((), ())), precision=FULL_P...  139 us
    all_gather x1, waiting for transfers between devices, body(): grads_whole = lax.all_gather(output_grads, 'col', axis=0, tiled=True)  127 us
    another operation x14, other arithmetic, orthogonalize(): lower_factor = jnp.linalg.cholesky(gram_matrix)  87.4 us
    dot_general x2, matrix products, contract_rows(): lax.dot_general(first, second, (((0,), (0,)), ((), ())), precision=FULL_P...  77.2 us
    dot_general x1, matrix products, body(): jnp.dot(buffer, factor_block, precision=FULL_PRECISION, preferred_element...  65.1 us
    reduce_scatter x1, waiting for transfers between devices, body(): lax.psum_scatter(contract_rows(buffer, ortho_left), 'row', scatter_dimens...  45.2 us
    another operation x3, other arithmetic, orthogonalize(): jax.scipy.linalg.solve_triangular(lower_factor, identity, lower=True)  40.3 us
  transfers between devices with their start and end apart: 7, of which 5 were waited for; matrix products, arithmetic and copies ran while one was open for 4% of the time, Pallas kernels for 0%

commit v1 on v0

--- a/solution.py
+++ b/solution.py
@@ -52,7 +52,7 @@
     left_partial = jnp.dot(
         buffer, factor_block, precision=FULL_PRECISION, preferred_element_type=jnp.float32
     )
-    left_factor = lax.psum(left_partial, "col")
+    left_factor = jnp.sum(lax.all_gather(left_partial, "col"), axis=0)
     gram_matrix = lax.psum(contract_rows(left_factor, left_factor), "row")
     ortho_left = orthogonalize(left_factor, gram_matrix)
     right_piece = lax.psum_scatter(

time: 1050 us -> 2070 us (1.97)
  waiting for transfers between devices: 514 us -> 1510 us
  other arithmetic: 134 us -> 159 us
    all_gather x0 -> x1, waiting for transfers between devices: none -> 1260 us  [body(): left_factor = jnp.sum(lax.all_gather(left_partial, 'col'), axis=0)]
    psum x1 -> x0, waiting for transfers between devices: 268 us -> none  [body(): left_factor = lax.psum(left_partial, 'col')]
    reduce_sum x0 -> x1, other arithmetic: none -> 24.8 us  [body(): left_factor = jnp.sum(lax.all_gather(left_partial, 'col'), axis=0)]
  transfers between devices with their start and end apart: 7 -> 7, of which waited for: 5 -> 5; matrix products, arithmetic and copies ran while one was open for 4% -> 2% of each run, Pallas kernels for 0% -> 0%
where the time goes in v1:
time: 2070 us
  waiting for transfers between devices  1510 us (73%)
  matrix products  323 us (16%)
  other arithmetic  159 us (8%)
  blocking collectives  39.7 us (2%)
    all_gather x1, waiting for transfers between devices, body(): left_factor = jnp.sum(lax.all_gather(left_partial, 'col'), axis=0)  1260 us
    dot_general x3, matrix products, outer_rows(): lax.dot_general(first, second, (((1,), (1,)), ((), ())), precision=FULL_P...  139 us
    all_gather x1, waiting for transfers between devices, body(): grads_whole = lax.all_gather(output_grads, 'col', axis=0, tiled=True)  127 us
    another operation x14, other arithmetic, orthogonalize(): lower_factor = jnp.linalg.cholesky(gram_matrix)  87.5 us
    dot_general x2, matrix products, contract_rows(): lax.dot_general(first, second, (((0,), (0,)), ((), ())), precision=FULL_P...  77.1 us
    dot_general x1, matrix products, body(): jnp.dot(buffer, factor_block, precision=FULL_PRECISION, preferred_element...  65.1 us
    reduce_scatter x1, waiting for transfers between devices, body(): lax.psum_scatter(contract_rows(buffer, ortho_left), 'row', scatter_dimens...  45.2 us
  transfers between devices with their start and end apart: 7, of which 5 were waited for; matrix products, arithmetic and copies ran while one was open for 2% of the time, Pallas kernels for 0%

profile of v1, /device:TPU:0, one launch (start us, length us, event | category | flops | bytes accessed | tf_op | source)
XLA Modules:
  0.0 2066.6 jit_solution(5031325351384720841)
XLA Ops:
  9.4 37.3 %all-gather.9.cloned.1.call-done = bf16[1024,2048]{1,0:T(8,128)(2,1)} async-done(((bf16[256,2048]{1,0:T(8,128)(2,1)}), bf16[1024,2048]{1,0:T(8,128)(2,1)}) %all-gather.9.cloned.1.call-update) | async-done | bytes 4194320 | tf_op jit(solution)/shard_map/all_gather | solution.py:46
  46.7 126.6 %all-gather.7.cloned.1.call-done = bf16[1024,4096]{1,0:T(8,128)(2,1)} async-done(((bf16[128,4096]{1,0:T(8,128)(2,1)}), bf16[1024,4096]{1,0:T(8,128)(2,1)}) %all-gather.7.cloned.1.call-update) | async-done | bytes 8388624 | tf_op jit(solution)/shard_map/all_gather | solution.py:43
  173.4 36.2 %convolution_add_fusion = f32[4096,2048]{1,0:T(8,128)} fusion(f32[4096,2048]{1,0:T(8,128)} %param.6, bf16[1024,4096]{1,0:T(8,128)(2,1)} %all-gather.7.cloned.1.call-done, bf16[1024,2048]{1,0:T(8,128)(2,1)} %all-gather.9.cloned.1.call-done), kind=kOutput, calls=%fused_computation.4 | convolution fusion | flops 17188257792 | bytes 79691776 | tf_op jit(solution)/shard_map/dot_general | solution.py:44
  209.6 65.1 %fusion.43 = f32[4096,512]{1,0:T(8,128)} fusion(f32[4096,2048]{1,0:T(8,128)} %convolution_add_fusion, f32[2048,512]{1,0:T(8,128)} %all-gather.11.cloned.1.call-done), kind=kOutput, calls=%fused_computation.85 | convolution fusion | flops 51539607552 | bytes 46137344 | tf_op jit(solution)/shard_map/dot_general | solution.py:52
  275.0 1264.7 %all-gather.15.cloned.1.call-done = f32[32768,512]{1,0:T(8,128)} async-done(((f32[4096,512]{1,0:T(8,128)}), f32[32768,512]{1,0:T(8,128)}) %all-gather.15.cloned.1.call-update) | async-done | bytes 67108880 | tf_op jit(solution)/shard_map/all_gather | solution.py:55
  1539.7 24.8 %reduce_sum.18 = f32[4096,512]{1,0:T(8,128)} reduce(f32[8,4096,512]{2,1,0:T(8,128)} %bitcast, f32[]{:T(128)} %constant.142.clone.1), dimensions={0}, to_apply=%region_0.0 | reduce | flops 14680064 | bytes 75497472 | tf_op jit(solution)/shard_map/reduce_sum | solution.py:55
  1564.5 18.4 fusion.44
  1583.9 35.4 %all-reduce.3.cloned.1.call-done = f32[512,512]{0,1:T(8,128)} async-done(((f32[512,512]{0,1:T(8,128)}), f32[512,512]{0,1:T(8,128)}) %all-reduce.3.cloned.1.call-update) | async-done | bytes 1048592 | tf_op jit(solution)/shard_map/psum | solution.py:56
  1622.4 11.7 cholesky.104
  1634.2 9.8 custom-call.31
  1644.7 11.7 cholesky.217
  1656.5 18.5 custom-call.32
  1675.7 11.7 cholesky.238
  1688.1 9.8 custom-call.33
  1698.6 11.7 cholesky.255
  1714.7 10.9 while.1
  1725.5 40.1 %custom-call.34 = f32[4,128,128]{1,2,0:T(8,128)S(1)} custom-call(f32[4,128,128]{2,1,0:T(8,128)} %get-tuple-element.10), custom_call_target="InvertDiagBlocksLowerTriangular" | custom-call | tf_op jit(solution)/shard_map/jit(_solve_triangular)/triangular_solve | solution.py:38
  1769.5 17.1 fusion.2
  1786.6 3.2 copy-done
  1789.8 58.7 %fusion.45 = f32[2048,512]{1,0:T(8,128)} fusion(f32[4096,2048]{1,0:T(8,128)} %convolution_add_fusion, f32[4096,512]{1,0:T(8,128)S(1)} %fusion.2), kind=kOutput, calls=%fused_computation.87 | convolution fusion | flops 51539607552 | bytes 46137344 | tf_op jit(solution)/shard_map/dot_general | solution.py:16
  1848.7 45.2 %reduce-scatter.2.cloned.1.call-done = f32[512,512]{1,0:T(8,128)} async-done(((f32[2048,512]{1,0:T(8,128)}), f32[512,512]{1,0:T(8,128)}) %reduce-scatter.2.cloned.1.call-update) | async-done | bytes 1048592 | tf_op jit(solution)/shard_map/reduce_scatter | solution.py:58
  1895.2 39.7 %psum.15 = f32[512]{0:T(512)S(1)} all-reduce(f32[512]{0:T(512)S(1)} %multiply_reduce_fusion), channel_id=1, replica_groups=mesh['row'=4,'col'=8] {'row','col'}, use_global_device_ids=true, to_apply=%region_12.13 | all-reduce | flops 512 | bytes 4096 | tf_op jit(solution)/shard_map/psum | solution.py:61
  1937.2 62.5 %multiply_subtract_fusion = f32[4096,2048]{1,0:T(8,128)} fusion(f32[4096,2048]{1,0:T(8,128)} %convolution_add_fusion, f32[4096,512]{1,0:T(8,128)} %copy-done, f32[2048,512]{1,0:T(8,128)} %all-gather.13.cloned.1.call-done), kind=kOutput, calls=%fused_computation.2 | convolution fusion | flops 51556384768 | bytes 79691776 | tf_op jit(solution)/shard_map/dot_general | solution.py:26
  1999.7 59.6 %subtract_convert_fusion = bf16[4096,2048]{1,0:T(8,128)(2,1)} fusion(bf16[4096,2048]{1,0:T(8,128)(2,1)} %param.5, f32[4096,512]{1,0:T(8,128)} %copy-done, f32[2048,512]{1,0:T(8,128)S(1)} %copy-done.1, f32[512]{0:T(512)S(1)} %add_sqrt_fusion), kind=kOutput, calls=%fused_computation.3 | convolution fusion | flops 51574210560 | bytes 46139392 | tf_op jit(solution)/shard_map/dot_general | solution.py:26
  (66 shorter events, 29.6 us)
Async XLA Ops:
  7.2 39.6 %all-gather.9.cloned.1.call-start = ((), (), s32[]{:S(2)}) async-start(), calls=%async_computation.2 | async-start | bytes 5242880 | tf_op jit(solution)/shard_map/all_gather | solution.py:46
  7.9 165.5 %all-gather.7.cloned.1.call-start = ((), (), s32[]{:S(2)}) async-start(), calls=%async_computation.1 | async-start | bytes 9437184 | tf_op jit(solution)/shard_map/all_gather | solution.py:43
  8.6 201.0 %all-gather.11.cloned.1.call-start = ((), (), s32[]{:S(2)}) async-start(), calls=%async_computation.3 | async-start | bytes 5242880 | tf_op jit(solution)/shard_map/all_gather | solution.py:51
  9.4 1530.3 %all-gather.15.cloned.1.call-start = ((), (), s32[]{:S(2)}) async-start(), calls=%async_computation.7 | async-start | bytes 75497472 | tf_op jit(solution)/shard_map/all_gather | solution.py:55
  274.7 1344.6 %all-reduce.3.cloned.1.call-start = ((), (), s32[]{:S(2)}) async-start(), calls=%async_computation.4 | async-start | bytes 2097152 | tf_op jit(solution)/shard_map/psum | solution.py:56
  1582.9 310.9 %reduce-scatter.2.cloned.1.call-start = ((), (), s32[]{:S(2)}) async-start(), calls=%async_computation.5 | async-start | bytes 5242880 | tf_op jit(solution)/shard_map/reduce_scatter | solution.py:58
  1786.6 3.2 copy-start
  1848.6 88.6 %all-gather.13.cloned.1.call-start = ((), (), s32[]{:S(2)}) async-start(), calls=%async_computation.6 | async-start | bytes 5242880 | tf_op jit(solution)/shard_map/all_gather | solution.py:64
  1937.2 62.5 %copy-start.1 = (f32[2048,512]{1,0:T(8,128)S(1)}, f32[2048,512]{1,0:T(8,128)}, u32[]{:S(2)}) copy-start(f32[2048,512]{1,0:T(8,128)} %all-gather.13.cloned.1.call-done) | copy-start | bytes 12582916
Sparse Core Ops, SparseCore 0:
  9.5 37.1 all-gather.8
  48.9 124.4 all-gather.6
  174.9 32.6 all-gather.10
  274.8 1264.7 all-gather.14
  1583.0 36.2 all-reduce.2
  1848.7 45.0 reduce-scatter.1
  1895.4 34.7 all-gather.12
